TPU v7x, 512 devices: a whole 4x4x16 slice. The times are simulated.
512 devices in a mesh: dp: 64 (over y_lo, z, core), mp: 8 (over y_hi, x).
Axes of the slice: x: 4, y: 4 (y_hi: 2, y_lo: 2; y = y_hi * 2 + y_lo), z: 16, core: 2. Of those that a mesh axis runs over, the one named last changes fastest.
Arguments:
- hidden_in: bfloat16 [32768, 4096], P('dp'), may hold values from -1.5 to 1.5
- w_query: bfloat16 [4096, 4096], P('dp', 'mp'), may hold values from -1 to 1
- w_key: bfloat16 [4096, 1024], P('dp', 'mp'), may hold values from -24 to 24
- w_value: bfloat16 [4096, 1024], P('dp', 'mp'), may hold values from -1 to 1
- w_out: bfloat16 [4096, 4096], P('dp', 'mp'), may hold values from -1 to 1
- value_weight: float32 [4096], P('mp'), may hold values from -0.09375 to 0.09375
- rewards: float32 [32768], P('dp'), may hold values from -0.6 to 0.6
- old_values: float32 [32768], P('dp'), may hold values from -6 to 6
- lengths: int32 [256], replicated, may hold values from 1 to 2048, 32768 in all
- terminal: int32 [256], replicated, may hold values 0 or 1
Outputs:
- value: float32 [32768], P('dp')
- advantage: float32 [32768], P('dp')
- value_loss: float32 [], replicated
All inputs are finite; a program needn't handle non-finite values.
Results may differ from a plain program's by a relative error of at most 0.012.
The roundings to bfloat16 on the way count: a program that leaves them out, or rounds other values in their place, can miss the bound.
Values may be sent and summed in bfloat16 or wider, within the bound.
A program may use at most 128 MiB of HBM per device.

v0:
```python
import jax
import jax.numpy as jnp
from jax import lax
from jax.sharding import PartitionSpec as P

HEAD = 128
discount = 0.999
trace_decay = 0.997
clip_range = 0.2
epsilon = 1e-05
rope_base = 500000.0


def sent_together(arrays, axis, dim, along):
    widths = [a.shape[along] for a in arrays]
    both = jnp.concatenate(arrays, axis=along)
    whole = lax.all_gather(both, axis, axis=dim, tiled=True)
    return tuple(jnp.split(whole, [sum(widths[:k]) for k in range(1, len(widths))], axis=along))


def from_everyone(array, axis):
    size = lax.axis_size(axis)
    return lax.all_to_all(
        jnp.broadcast_to(array[None], (size, *array.shape)), axis, 0, 0, tiled=True
    )


def of_everyone(array, axis):
    everything = from_everyone(array, axis)
    return jnp.sum(everything, axis=0)


def in_one(arrays, axis):
    ends = [0]
    for a in arrays:
        ends.append(ends[-1] + a.size)
    total = of_everyone(jnp.concatenate([a.ravel() for a in arrays]), axis)
    return tuple((total[b:e].reshape(a.shape) for a, b, e in zip(arrays, ends, ends[1:])))


def from_behind(array, axis, by):
    size = lax.axis_size(axis)
    pairs = [(i, i + by) for i in range(size) if 0 <= i + by < size]
    return lax.ppermute(array, axis, pairs)


def collected_together(array, axis):
    leaves = jax.tree.leaves(array)
    order = sorted(range(len(leaves)), key=lambda k: -leaves[k].size)
    width = (1, *leaves[order[0]].shape)[-1]
    lines = [
        jnp.pad(leaves[k].reshape(-1), (0, -leaves[k].size % width)).reshape(-1, width)
        for k in order
    ]
    both, at, found = (from_everyone(jnp.concatenate(lines), axis), 0, {})
    for k, line in zip(order, lines):
        slab = both[:, at : at + len(line)].reshape(len(both), -1)
        found[k] = slab[:, : leaves[k].size].reshape(-1, *leaves[k].shape)
        at += len(line)
    numbers = iter(range(len(leaves)))
    return jax.tree.map(lambda _: found[next(numbers)], array)


def joined_by_halves(pieces, combine):
    while len(jax.tree.leaves(pieces)[0]) > 1:
        pieces = jax.vmap(combine)(
            *(jax.tree.map(lambda part: part[side::2], pieces) for side in (0, 1))
        )
    return jax.tree.map(lambda part: part[0], pieces)


def prefix_2(array, axis, combine, identity):
    size, mine = (lax.axis_size(axis), lax.axis_index(axis))
    passed = jnp.arange(size) > mine

    def kept(part, zero, own):
        part = jnp.where(
            passed.reshape(-1, *(1 for _ in own.shape)), part, jnp.asarray(zero, own.dtype)
        )
        return part[::-1]

    pieces = collected_together(array, axis)
    return joined_by_halves(jax.tree.map(kept, pieces, identity, array), combine)


def rotate(states, positions):
    half = HEAD // 2
    freq = rope_base ** (-jnp.arange(half, dtype=jnp.float32) * 2.0 / HEAD)
    angles = positions[:, None] * freq[None, :]
    cosine = jnp.cos(angles)[:, None, :]
    sine = jnp.sin(angles)[:, None, :]
    first = states[..., :half]
    second = states[..., half:]
    return jnp.concatenate([first * cosine - second * sine, second * cosine + first * sine], -1)


def body(
    hidden_in, w_query, w_key, w_value, w_out, value_weight, rewards, old_values, lengths, terminal
):
    rows = hidden_in.shape[0]
    width = hidden_in.shape[1]
    states = hidden_in.astype(jnp.float32)
    normed = (states * lax.rsqrt(jnp.mean(states * states, 1, keepdims=True) + epsilon)).astype(
        jnp.bfloat16
    )
    pieces = sent_together((w_query, w_key, w_value, w_out), "dp", 0, 1)
    add_pieces = pieces[:3]
    summed = tuple(
        (jnp.dot(normed, piece, preferred_element_type=jnp.float32) for piece in add_pieces)
    )
    stored = pieces[3]
    query_sum, key_sum, value_sum, whole_out = summed + (stored,)
    position_ids = lax.axis_index("dp") * rows + jnp.arange(rows, dtype=jnp.int32)
    positions = position_ids.astype(jnp.float32)
    local_heads = w_query.shape[1] // HEAD
    local_kv = w_key.shape[1] // HEAD
    group = local_heads // local_kv
    query = rotate(query_sum.reshape(rows, local_heads, HEAD), positions).astype(jnp.bfloat16)
    key = rotate(key_sum.reshape(rows, local_kv, HEAD), positions).astype(jnp.bfloat16)
    values_proj = value_sum.astype(jnp.bfloat16).reshape(rows, local_kv, HEAD)
    ends = jnp.cumsum(lengths)
    matches = ends[None, :] - 1 == position_ids[:, None]
    finished = jnp.any(matches, 1).astype(jnp.float32)
    stopped = jnp.sum(jnp.where(matches, terminal[None, :], 0), 1).astype(jnp.float32)
    episode = jnp.sum((ends[None, :] <= position_ids[:, None]).astype(jnp.int32), 1)
    order = jnp.arange(rows, dtype=jnp.int32)
    same_episode = episode[None, :] == episode[:, None]
    allowed = (order[None, :] <= order[:, None]) & same_episode
    scores = jnp.einsum(
        "tkgd,skd->kgts",
        query.reshape(rows, local_kv, group, HEAD),
        key,
        preferred_element_type=jnp.float32,
    ) * (1.0 / HEAD**0.5)
    masked = jnp.where(allowed[None, None], scores, -1e30)
    largest = jnp.max(masked, -1, keepdims=True)
    expon = jnp.where(allowed[None, None], jnp.exp(masked - largest), 0.0)
    probs = (expon / jnp.sum(expon, -1, keepdims=True)).astype(jnp.bfloat16)
    output = jnp.einsum("kgts,skd->tkgd", probs, values_proj, preferred_element_type=jnp.float32)
    attended = output.astype(jnp.bfloat16).reshape(rows, local_heads * HEAD)
    all_heads = lax.all_gather(attended, "mp", axis=1, tiled=True)
    projected = jnp.dot(all_heads, whole_out, preferred_element_type=jnp.float32)
    feature_count = w_out.shape[1]
    own_states = lax.dynamic_slice_in_dim(
        states, lax.axis_index("mp") * feature_count, feature_count, 1
    )
    residual = own_states + projected
    square_sum, head_sum = in_one(
        (jnp.sum(residual * residual, 1), jnp.sum(residual * value_weight[None, :], 1)), "mp"
    )
    value = head_sum * lax.rsqrt(square_sum / width + epsilon)
    following = from_behind(old_values[:1], "dp", -1)
    next_old = jnp.concatenate([old_values[1:], following])
    booted = jnp.where(finished > 0, (1.0 - stopped) * old_values, next_old)
    delta = rewards + discount * booted - old_values
    keep_rate = discount * trace_decay
    spacing = (order[None, :] - order[:, None]).astype(jnp.float32)
    forward_mask = (spacing >= 0.0) & same_episode
    decay_matrix = jnp.where(
        forward_mask, jnp.power(jnp.float32(keep_rate), jnp.maximum(spacing, 0.0)), 0.0
    )
    local_part = jnp.dot(decay_matrix, delta, precision=lax.Precision.HIGHEST)
    remaining = (rows - order).astype(jnp.float32)
    reach = jnp.where(episode == episode[-1], jnp.power(jnp.float32(keep_rate), remaining), 0.0) * (
        1.0 - finished[-1]
    )

    def compose(earlier, later_map):
        return (later_map[0] + later_map[1] * earlier[0], later_map[1] * earlier[1])

    prefix = prefix_2(
        (local_part[:1], reach[:1]),
        "dp",
        compose,
        (jnp.zeros((1,), jnp.float32), jnp.ones((1,), jnp.float32)),
    )
    incoming = prefix[0][0]
    advantage = local_part + reach * incoming
    returns = advantage + old_values
    clipped = old_values + jnp.clip(value - old_values, -clip_range, clip_range)
    terms = jnp.maximum((value - returns) ** 2, (clipped - returns) ** 2)
    total_loss = of_everyone(jnp.sum(terms), "dp")
    value_loss = 0.5 * total_loss / (rows * lax.axis_size("dp"))
    return (value, advantage, value_loss)


def solution(mesh):
    return jax.shard_map(
        body,
        mesh=mesh,
        in_specs=(
            P("dp", None),
            P("dp", "mp"),
            P("dp", "mp"),
            P("dp", "mp"),
            P("dp", "mp"),
            P("mp"),
            P("dp"),
            P("dp"),
            P(),
            P(),
        ),
        out_specs=(P("dp"), P("dp"), P()),
        check_vma=False,
    )
```

profile of v0, /device:TPU:1, one launch (start us, length us, event | category | flops | bytes accessed | tf_op | source)
XLA Modules:
  0.0 308.6 jit_solution(11443152681858207137)
XLA Ops:
  7.2 1.6 pad_maximum_fusion
  8.9 1.0 reduce-window.9
  10.0 6.5 %copy.47 = bf16[512,4096]{0,1:T(8,128)(2,1)} copy(bf16[512,4096]{1,0:T(8,128)(2,1)} %param.10) | data formatting | bytes 8388608 | tf_op args[0]
  16.5 0.1 slice_reduce_fusion.2
  16.7 0.3 fusion.29
  17.0 3.1 %multiply_reduce_fusion = f32[512]{0:T(512)S(1)} fusion(bf16[512,4096]{0,1:T(8,128)(2,1)} %copy.47), kind=kLoop, calls=%fused_computation.1 | loop fusion | flops 6290944 | bytes 4196352 | tf_op jit(solution)/shard_map/reduce_sum | solution.py:103
  20.2 0.2 compare_and_fusion.1
  20.4 1.0 multiply_cosine_fusion
  21.4 125.4 %all-gather.3.cloned.1.call-done = bf16[4096,1280]{1,0:T(8,128)(2,1)} async-done(((bf16[64,1280]{1,0:T(8,128)(2,1)}), bf16[4096,1280]{1,0:T(8,128)(2,1)}) %all-gather.3.cloned.1.call-update) | async-done | bytes 10485776 | tf_op jit(solution)/shard_map/all_gather | solution.py:17
  146.8 3.6 %fusion.17 = f32[512,1,128]{0,2,1:T(8,128)S(1)} fusion(f32[512]{0:T(512)S(1)} %add_rsqrt_fusion, bf16[512,4096]{0,1:T(8,128)(2,1)} %copy.47, bf16[4096,1280]{1,0:T(8,128)(2,1)} %all-gather.3.cloned.1.call-done), kind=kOutput, calls=%fused_computation.20 | convolution fusion | flops 543162368 | bytes 5507072 | tf_op jit(solution)/shard_map/dot_general | solution.py:109
  150.4 0.6 fusion.49
  151.0 4.7 %fusion.2 = f32[512,512]{0,1:T(8,128)S(1)} fusion(bf16[4096,1280]{1,0:T(8,128)(2,1)} %all-gather.3.cloned.1.call-done, f32[512]{0:T(512)S(1)} %add_rsqrt_fusion, bf16[512,4096]{0,1:T(8,128)(2,1)S(1)} %copy-done), kind=kOutput, calls=%fused_computation.4 | convolution fusion | flops 2153775104 | bytes 9439232 | tf_op jit(solution)/shard_map/dot_general | solution.py:109
  155.7 0.1 fusion.60
  155.8 0.3 copy.63
  156.1 0.3 copy.62
  156.5 0.3 subtract_convert_fusion
  156.8 1.2 fusion.4
  158.0 2.1 copy-done.1
  160.1 1.0 fusion.7
  161.1 7.6 %fusion.14 = bf16[128,4,512]{2,0,1:T(8,128)(2,1)} fusion(f32[4,512]{1,0:T(4,128)S(1)} %fusion.7, f32[4,512]{1,0:T(4,128)S(1)} %get-tuple-element.34, f32[512,512,4]{1,0,2:T(8,128)} %copy-done.1, pred[512,512]{0,1:T(8,128)(4,1)S(1)} %compare_and_fusion.1, f32[512]{0:T(512)S(1)} %copy-done.4, bf16[512,4096]{0,1:T(8,128)(2,1)} %copy.47, ...), kind=kOutput, calls=%fused_computation.19 | convolution fusion | flops 818216960 | bytes 10242048 | tf_op jit(solution)/shard_map/kgts,skd->tkgd/dot_general | solution.py:139
  168.8 0.5 slice.142
  169.3 2.2 collective-permute-start
  171.5 0.7 slice.143
  172.3 0.2 compare_reduce_fusion
  172.5 0.6 slice.144
  173.7 0.7 select_multiply_fusion
  174.4 0.5 slice.146
  175.0 0.7 fusion.52
  175.7 1.1 fusion.22
  176.8 0.5 slice.145
  177.3 1.4 maximum_bitcast_fusion.2
  178.7 0.6 broadcast_in_dim.56
  179.3 9.7 %all-to-all-start.1 = ((f32[64,2,1]{1,2,0:T(1,128)}), f32[64,2,1]{1,2,0:T(1,128)S(1)}, u32[]{:S(2)}, u32[]{:S(2)}) async-start(f32[64,2,1]{1,2,0:T(1,128)} %broadcast_in_dim.56), calls=%async_computation.1 | async-start | bytes 65536 | tf_op jit(solution)/shard_map/all_to_all | solution.py:23
  189.0 6.7 %convert_element_type.52 = f32[512,4096]{0,1:T(8,128)} convert(bf16[512,4096]{0,1:T(8,128)(2,1)} %copy.47) | non-fusion elementwise | flops 2097152 | bytes 12582912 | tf_op jit(solution)/shard_map/convert_element_type | solution.py:102
  195.8 6.6 %all-to-all-done.1 = f32[64,2,1]{1,2,0:T(1,128)S(1)} async-done(((f32[64,2,1]{1,2,0:T(1,128)}), f32[64,2,1]{1,2,0:T(1,128)S(1)}, u32[]{:S(2)}, u32[]{:S(2)}) %all-to-all-start.1) | async-done | bytes 544 | tf_op jit(solution)/shard_map/all_to_all | solution.py:23
  202.3 1.1 slice_reduce_fusion
  203.4 0.1 slice.156
  203.6 0.1 slice.151
  203.7 0.1 slice.153
  203.8 0.1 slice.148
  203.9 0.1 slice.152
  204.0 0.1 slice.157
  204.1 0.1 slice.149
  204.2 0.1 slice.154
  204.3 0.1 slice.161
  204.4 0.1 slice.158
  204.6 0.1 slice.159
  204.7 0.1 slice.155
  204.8 0.1 slice.165
  204.9 0.1 slice.162
  205.0 0.1 slice.163
  205.1 0.1 slice.160
  205.3 0.1 slice.166
  206.0 45.3 %all-gather.5.cloned.1.call-done = bf16[512,4096]{0,1:T(8,128)(2,1)} async-done(((bf16[512,512]{0,1:T(8,128)(2,1)}), bf16[512,4096]{0,1:T(8,128)(2,1)}) %all-gather.5.cloned.1.call-update) | async-done | bytes 4194320 | tf_op jit(solution)/shard_map/all_gather | solution.py:141
  251.3 6.1 %multiply_reduce_fusion.2 = (f32[512]{0:T(512)S(1)}, f32[512]{0:T(512)S(1)}) fusion(f32[512]{0:T(512)S(1)} %copy-done.7, bf16[512,4096]{0,1:T(8,128)(2,1)} %all-gather.5.cloned.1.call-done, bf16[4096,1280]{1,0:T(8,128)(2,1)} %all-gather.3.cloned.1.call-done, f32[512,4096]{0,1:T(8,128)} %convert_element_type.52, s32[]{:T(128)S(6)} %select_n.49), kind=kOutput, calls=%fused_computation.33 | convolution fusion | flops 2148793344 | bytes 9443332 | tf_op jit(solution)/shard_map/dot_general | solution.py:142
  257.4 0.6 broadcast_in_dim.51
  258.0 3.3 %all-to-all-start = ((f32[8,1,1024]{2,1,0:T(1,128)}), f32[8,1,1024]{2,1,0:T(1,128)S(1)}, u32[]{:S(2)}, u32[]{:S(2)}) async-start(f32[8,1,1024]{2,1,0:T(1,128)} %broadcast_in_dim.51), calls=%async_computation | async-start | bytes 65536 | tf_op jit(solution)/shard_map/all_to_all | solution.py:23
  261.4 0.6 fusion.61
  262.0 0.6 slice.174
  264.5 3.4 %all-to-all-done = f32[8,1,1024]{2,1,0:T(1,128)S(1)} async-done(((f32[8,1,1024]{2,1,0:T(1,128)}), f32[8,1,1024]{2,1,0:T(1,128)S(1)}, u32[]{:S(2)}, u32[]{:S(2)}) %all-to-all-start) | async-done | bytes 32800 | tf_op jit(solution)/shard_map/all_to_all | solution.py:23
  268.0 2.0 maximum_reduce_fusion
  269.9 0.7 broadcast_in_dim.96
  270.6 28.7 %all_to_all.17 = f32[64,1,1]{2,1,0:T(1,128)S(1)} all-to-all(f32[64,1,1]{2,1,0:T(1,128)S(1)} %broadcast_in_dim.96), channel_id=1, replica_groups=mesh['dp'=64,'mp'=8] {'dp'}, dimensions={0} | all-to-all | bytes 512 | tf_op jit(solution)/shard_map/all_to_all | solution.py:23
  299.3 0.7 reduce_sum.89
  (44 shorter events, 1.2 us)
Async XLA Ops:
  7.2 139.6 %all-gather.3.cloned.1.call-start = ((), (), s32[]{:S(2)}) async-start(), calls=%async_computation.3 | async-start | bytes 10649600 | tf_op jit(solution)/shard_map/all_gather | solution.py:17
  8.8 242.5 %all-gather.5.cloned.1.call-start = ((), (), s32[]{:S(2)}) async-start(), calls=%async_computation.4 | async-start | bytes 4718592 | tf_op jit(solution)/shard_map/all_gather | solution.py:141
  10.0 6.7 %copy-start.6 = (s32[256]{0:T(256)S(1)}, s32[256]{0:T(256)}, u32[]{:S(2)}) copy-start(s32[256]{0:T(256)} %param.19) | copy-start | bytes 3076
  20.1 130.8 %copy-start.3 = (f32[512]{0:T(512)}, f32[512]{0:T(512)S(1)}, u32[]{:S(2)}) copy-start(f32[512]{0:T(512)S(1)} %add_rsqrt_fusion) | copy-start | bytes 6148
  146.8 4.2 %copy-start = (bf16[512,4096]{0,1:T(8,128)(2,1)S(1)}, bf16[512,4096]{0,1:T(8,128)(2,1)}, u32[]{:S(2)}) copy-start(bf16[512,4096]{0,1:T(8,128)(2,1)} %copy.47) | copy-start | bytes 12582916
  156.8 4.4 %copy-start.4 = (f32[512]{0:T(512)S(1)}, f32[512]{0:T(512)}, u32[]{:S(2)}) copy-start(f32[512]{0:T(512)} %copy-done.3) | copy-start | bytes 6148
  158.0 2.1 copy-start.1
  161.1 7.7 %copy-start.2 = (f32[512]{0:T(512)S(1)}, f32[512]{0:T(512)}, u32[]{:S(2)}) copy-start(f32[512]{0:T(512)} %param.17) | copy-start | bytes 6148
  161.1 13.8 %copy-start.5 = (f32[512]{0:T(512)S(1)}, f32[512]{0:T(512)}, u32[]{:S(2)}) copy-start(f32[512]{0:T(512)} %param.16) | copy-start | bytes 6148
  169.3 5.6 %collective-permute-start = (f32[1]{0:T(128)}, f32[1]{0:T(128)}, u32[]{:S(2)}, u32[]{:S(2)}) collective-permute-start(f32[1]{0:T(128)} %slice.142), channel_id=1, source_target_pairs={{8,0},{16,8},{24,16},{32,24},{40,32},{48,40},{56,48},{64,56},{72,6... | collective-permute-start | bytes 20 | tf_op jit(solution)/shard_map/ppermute | solution.py:44
  179.3 23.1 %all-to-all-start.1 = ((f32[64,2,1]{1,2,0:T(1,128)}), f32[64,2,1]{1,2,0:T(1,128)S(1)}, u32[]{:S(2)}, u32[]{:S(2)}) async-start(f32[64,2,1]{1,2,0:T(1,128)} %broadcast_in_dim.56), calls=%async_computation.1 | async-start | bytes 65536 | tf_op jit(solution)/shard_map/all_to_all | solution.py:23
  189.0 62.3 %copy-start.7 = (f32[512]{0:T(512)S(1)}, f32[512]{0:T(512)}, u32[]{:S(2)}) copy-start(f32[512]{0:T(512)} %param.15) | copy-start | bytes 6148
  258.0 9.9 %all-to-all-start = ((f32[8,1,1024]{2,1,0:T(1,128)}), f32[8,1,1024]{2,1,0:T(1,128)S(1)}, u32[]{:S(2)}, u32[]{:S(2)}) async-start(f32[8,1,1024]{2,1,0:T(1,128)} %broadcast_in_dim.51), calls=%async_computation | async-start | bytes 65536 | tf_op jit(solution)/shard_map/all_to_all | solution.py:23
Sparse Core Ops, SparseCore 0:
  10.1 136.5 all-gather.2
  168.9 82.2 all-gather.4
where the time goes:
time: 309 us
  waiting for transfers between devices  181 us (59%)
  blocking collectives  28.7 us (9%)
  matrix products  24.4 us (8%)
  other arithmetic  21.7 us (7%)
  local copies, waits for them, and re-layouts  19.1 us (6%)
  between operations  18.7 us (6%)
  starting transfers between devices  15.3 us (5%)
    all_gather x1, waiting for transfers between devices, sent_together(): whole = lax.all_gather(both, axis, axis=dim, tiled=True)  125 us
    all_gather x1, waiting for transfers between devices, body(): all_heads = lax.all_gather(attended, 'mp', axis=1, tiled=True)  45.3 us
    all_to_all x1, blocking collectives, from_everyone(): lax.all_to_all(jnp.broadcast_to(array[None], (size, *array.shape)), axis,...  28.7 us
    all_to_all x2, starting transfers between devices, from_everyone(): lax.all_to_all(jnp.broadcast_to(array[None], (size, *array.shape)), axis,...  13.1 us
    all_to_all x2, waiting for transfers between devices, from_everyone(): lax.all_to_all(jnp.broadcast_to(array[None], (size, *array.shape)), axis,...  9.99 us
    unnamed x19, local copies, waits for them, and re-layouts  9.27 us
    dot_general x2, matrix products, body(): jnp.dot(normed, piece, preferred_element_type=jnp.float32)  8.31 us
    dot_general x1, matrix products, body(): jnp.einsum('kgts,skd->tkgd', probs, values_proj, preferred_element_type=j...  7.65 us
  transfers between devices with their start and end apart: 5, of which 4 were waited for; matrix products, arithmetic and copies ran while one was open for 10% of the time, Pallas kernels for 0%

commit v1 on v0

--- a/solution.py
+++ b/solution.py
@@ -138,7 +138,12 @@
     probs = (expon / jnp.sum(expon, -1, keepdims=True)).astype(jnp.bfloat16)
     output = jnp.einsum("kgts,skd->tkgd", probs, values_proj, preferred_element_type=jnp.float32)
     attended = output.astype(jnp.bfloat16).reshape(rows, local_heads * HEAD)
-    all_heads = lax.all_gather(attended, "mp", axis=1, tiled=True)
+    all_rows = []
+    for _ in range(lax.axis_size("mp")):
+        all_rows.append(attended)
+    latest = jnp.stack(all_rows, axis=0)
+    frame_out = lax.all_to_all(latest, axis_name="mp", split_axis=0, concat_axis=0)
+    all_heads = jnp.concatenate(frame_out, axis=1)
     projected = jnp.dot(all_heads, whole_out, preferred_element_type=jnp.float32)
     feature_count = w_out.shape[1]
     own_states = lax.dynamic_slice_in_dim(

time: 309 us -> 296 us (0.958)
  waiting for transfers between devices: 181 us -> 140 us
  starting transfers between devices: 15.3 us -> 42.8 us
  blocking collectives: 28.7 us -> 23.9 us
  local copies, waits for them, and re-layouts: 19.1 us -> 22.8 us
    all_gather x1 -> x0, waiting for transfers between devices: 45.3 us -> none  [body(): all_heads = lax.all_gather(attended, 'mp', axis=1, tiled=True)]
    all_to_all x0 -> x1, waiting for transfers between devices: none -> 40.8 us  [body(): lax.all_to_all(latest, axis_name='mp', split_axis=0, concat_axis=0)]
    all_gather x1, waiting for transfers between devices: 125 us -> 95.9 us  [sent_together(): whole = lax.all_gather(both, axis, axis=dim, tiled=True)]
    all_to_all x2, starting transfers between devices: 13.1 us -> 27.9 us  [from_everyone(): lax.all_to_all(jnp.broadcast_to(array[None], (size, *array.shape)), axis,...]
    ppermute x1, starting transfers between devices: 2.18 us -> 8.74 us  [from_behind(): return lax.ppermute(array, axis, pairs)]
    all_to_all x2, waiting for transfers between devices: 9.99 us -> 3.51 us  [from_everyone(): lax.all_to_all(jnp.broadcast_to(array[None], (size, *array.shape)), axis,...]
    all_to_all x0 -> x1, starting transfers between devices: none -> 6.11 us  [body(): lax.all_to_all(latest, axis_name='mp', split_axis=0, concat_axis=0)]
    all_to_all x1, blocking collectives: 28.7 us -> 23.9 us  [from_everyone(): lax.all_to_all(jnp.broadcast_to(array[None], (size, *array.shape)), axis,...]
  transfers between devices with their start and end apart: 5 -> 5, of which waited for: 4 -> 3; matrix products, arithmetic and copies ran while one was open for 10% -> 18% of each run, Pallas kernels for 0% -> 0%
where the time goes in v1:
time: 296 us; the launch traced here: 295 us
  waiting for transfers between devices  140 us (47%)
  starting transfers between devices  42.8 us (14%)
  matrix products  24.2 us (8%)
  blocking collectives  23.9 us (8%)
  other arithmetic  22.9 us (8%)
  local copies, waits for them, and re-layouts  22.8 us (8%)
  between operations  18.6 us (6%)
    all_gather x1, waiting for transfers between devices, sent_together(): whole = lax.all_gather(both, axis, axis=dim, tiled=True)  95.9 us
    all_to_all x1, waiting for transfers between devices, body(): lax.all_to_all(latest, axis_name='mp', split_axis=0, concat_axis=0)  40.8 us
    all_to_all x2, starting transfers between devices, from_everyone(): lax.all_to_all(jnp.broadcast_to(array[None], (size, *array.shape)), axis,...  27.9 us
    all_to_all x1, blocking collectives, from_everyone(): lax.all_to_all(jnp.broadcast_to(array[None], (size, *array.shape)), axis,...  23.9 us
    unnamed x13, local copies, waits for them, and re-layouts  9.23 us
    ppermute x1, starting transfers between devices, from_behind(): return lax.ppermute(array, axis, pairs)  8.74 us
    dot_general x2, matrix products, body(): jnp.dot(normed, piece, preferred_element_type=jnp.float32)  8.3 us
    convert_element_type x1, other arithmetic, body(): states = hidden_in.astype(jnp.float32)  6.73 us
  transfers between devices with their start and end apart: 5, of which 3 were waited for; matrix products, arithmetic and copies ran while one was open for 18% of the time, Pallas kernels for 0%

profile of v1, /device:TPU:1, one launch (start us, length us, event | category | flops | bytes accessed | tf_op | source)
XLA Modules:
  0.0 295.5 jit_solution(449109743966171744)
XLA Ops:
  7.2 1.6 pad_maximum_fusion
  8.8 1.2 slice.142
  10.0 8.7 %collective-permute-start = (f32[1]{0:T(128)}, f32[1]{0:T(128)}, u32[]{:S(2)}, u32[]{:S(2)}) collective-permute-start(f32[1]{0:T(128)} %slice.142), channel_id=1, source_target_pairs={{8,0},{16,8},{24,16},{32,24},{40,32},{48,40},{56,48},{64,56},{72,6... | collective-permute-start | bytes 20 | tf_op jit(solution)/shard_map/ppermute | solution.py:44
  18.8 0.8 slice.141
  19.5 1.0 reduce-window.9
  20.6 0.1 slice_reduce_fusion.2
  20.8 1.0 fusion.29
  21.8 0.7 slice.143
  22.4 0.2 compare_reduce_fusion
  22.7 0.6 slice.144
  23.9 0.6 select_multiply_fusion
  24.6 0.5 slice.146
  25.1 6.5 %copy.48 = bf16[512,4096]{0,1:T(8,128)(2,1)} copy(bf16[512,4096]{1,0:T(8,128)(2,1)} %param.10) | data formatting | bytes 8388608 | tf_op args[0]
  31.6 3.2 %multiply_reduce_fusion = f32[512]{0:T(512)S(1)} fusion(bf16[512,4096]{0,1:T(8,128)(2,1)} %copy.48), kind=kLoop, calls=%fused_computation.1 | loop fusion | flops 6290944 | bytes 4196352 | tf_op jit(solution)/shard_map/reduce_sum | solution.py:103
  34.8 0.2 compare_and_fusion.1
  35.1 1.0 multiply_cosine_fusion
  36.1 0.6 fusion.52
  36.7 1.1 fusion.22
  37.8 0.5 slice.145
  38.4 1.4 maximum_bitcast_fusion.2
  39.7 0.6 broadcast_in_dim.56
  40.3 11.3 %all-to-all-start.2 = ((f32[64,2,1]{1,2,0:T(1,128)}), f32[64,2,1]{1,2,0:T(1,128)S(1)}, u32[]{:S(2)}, u32[]{:S(2)}) async-start(f32[64,2,1]{1,2,0:T(1,128)} %broadcast_in_dim.56), calls=%async_computation.2 | async-start | bytes 65536 | tf_op jit(solution)/shard_map/all_to_all | solution.py:23
  51.7 95.9 %all-gather.2.cloned.1.call-done = bf16[4096,1280]{1,0:T(8,128)(2,1)} async-done(((bf16[64,1280]{1,0:T(8,128)(2,1)}), bf16[4096,1280]{1,0:T(8,128)(2,1)}) %all-gather.2.cloned.1.call-update) | async-done | bytes 10485776 | tf_op jit(solution)/shard_map/all_gather | solution.py:17
  147.6 3.6 %fusion.17 = f32[512,1,128]{0,2,1:T(8,128)S(1)} fusion(f32[512]{0:T(512)S(1)} %add_rsqrt_fusion, bf16[512,4096]{0,1:T(8,128)(2,1)} %copy.48, bf16[4096,1280]{1,0:T(8,128)(2,1)} %all-gather.2.cloned.1.call-done), kind=kOutput, calls=%fused_computation.20 | convolution fusion | flops 543162368 | bytes 5507072 | tf_op jit(solution)/shard_map/dot_general | solution.py:109
  151.2 1.2 fusion.49
  152.4 4.7 %fusion.2 = f32[512,512]{0,1:T(8,128)S(1)} fusion(bf16[4096,1280]{1,0:T(8,128)(2,1)} %all-gather.2.cloned.1.call-done, f32[512]{0:T(512)S(1)} %add_rsqrt_fusion, bf16[512,4096]{0,1:T(8,128)(2,1)S(1)} %copy-done), kind=kOutput, calls=%fused_computation.4 | convolution fusion | flops 2153775104 | bytes 9439232 | tf_op jit(solution)/shard_map/dot_general | solution.py:109
  157.1 0.1 fusion.60
  157.2 0.3 copy.64
  157.5 0.3 copy.63
  157.9 0.3 subtract_convert_fusion
  158.2 2.0 fusion.4
  160.2 2.1 copy-done.1
  162.3 1.0 fusion.7
  163.3 6.6 %fusion.14 = bf16[128,4,512]{2,0,1:T(8,128)(2,1)S(1)} fusion(f32[4,512]{1,0:T(4,128)S(1)} %fusion.7, f32[4,512]{1,0:T(4,128)S(1)} %get-tuple-element.34, f32[512,512,4]{1,0,2:T(8,128)} %copy-done.1, pred[512,512]{0,1:T(8,128)(4,1)S(1)} %compare_and_fusion.1, f32[512]{0:T(512)S(1)} %add_rsqrt_fusion, bf16[512,4096]{0,1:T(8,128)(2,1)} %copy.48, ...), kind=kOutput, calls=%fused_computation.19 | convolution fusion | flops 818216960 | bytes 10242048 | tf_op jit(solution)/shard_map/kgts,skd->tkgd/dot_general | solution.py:139
  170.0 2.4 stack.3
  172.4 6.1 %all-to-all-start = ((bf16[8,512,512]{1,2,0:T(8,128)(2,1)}), bf16[8,512,512]{1,2,0:T(8,128)(2,1)}, u32[]{:S(2)}, u32[]{:S(2)}) async-start(bf16[8,512,512]{1,2,0:T(8,128)(2,1)} %stack.3), calls=%async_computation | async-start | bytes 8388608 | tf_op jit(solution)/shard_map/all_to_all | solution.py:145
  178.5 6.7 %convert_element_type.52 = f32[512,4096]{0,1:T(8,128)} convert(bf16[512,4096]{0,1:T(8,128)(2,1)} %copy.48) | non-fusion elementwise | flops 2097152 | bytes 12582912 | tf_op jit(solution)/shard_map/convert_element_type | solution.py:102
  185.2 1.1 slice_reduce_fusion
  186.4 0.1 slice.156
  186.5 0.1 slice.151
  186.6 0.1 slice.153
  186.7 0.1 slice.148
  186.9 0.1 slice.152
  187.0 0.1 slice.157
  187.1 0.1 slice.149
  187.1 0.1 slice.154
  187.2 0.1 slice.161
  187.4 0.1 slice.158
  187.5 0.1 slice.159
  187.6 0.1 slice.155
  187.7 0.1 slice.165
  187.8 0.1 slice.162
  188.0 0.1 slice.160
  188.9 40.8 %all-to-all-done = bf16[8,512,512]{1,2,0:T(8,128)(2,1)} async-done(((bf16[8,512,512]{1,2,0:T(8,128)(2,1)}), bf16[8,512,512]{1,2,0:T(8,128)(2,1)}, u32[]{:S(2)}, u32[]{:S(2)}) %all-to-all-start) | async-done | bytes 4194336 | tf_op jit(solution)/shard_map/all_to_all | solution.py:145
  229.7 6.1 %multiply_reduce_fusion.2 = (f32[512]{0:T(512)S(1)}, f32[512]{0:T(512)S(1)}) fusion(f32[512]{0:T(512)S(1)} %copy-done.4, bf16[512,4096]{0,1:T(8,128)(2,1)} %bitcast.15, bf16[4096,1280]{1,0:T(8,128)(2,1)} %all-gather.2.cloned.1.call-done, f32[512,4096]{0,1:T(8,128)} %convert_element_type.52, s32[]{:T(128)S(6)} %select_n.49), kind=kOutput, calls=%fused_computation.33 | convolution fusion | flops 2148793344 | bytes 9443332 | tf_op jit(solution)/shard_map/dot_general | solution.py:147
  235.8 0.6 broadcast_in_dim.51
  236.5 16.6 %all-to-all-start.1 = ((f32[8,1,1024]{2,1,0:T(1,128)}), f32[8,1,1024]{2,1,0:T(1,128)S(1)}, u32[]{:S(2)}, u32[]{:S(2)}) async-start(f32[8,1,1024]{2,1,0:T(1,128)} %broadcast_in_dim.51), calls=%async_computation.1 | async-start | bytes 65536 | tf_op jit(solution)/shard_map/all_to_all | solution.py:23
  253.1 0.6 fusion.61
  253.6 0.6 slice.174
  256.2 3.5 %all-to-all-done.1 = f32[8,1,1024]{2,1,0:T(1,128)S(1)} async-done(((f32[8,1,1024]{2,1,0:T(1,128)}), f32[8,1,1024]{2,1,0:T(1,128)S(1)}, u32[]{:S(2)}, u32[]{:S(2)}) %all-to-all-start.1) | async-done | bytes 32800 | tf_op jit(solution)/shard_map/all_to_all | solution.py:23
  259.7 1.9 maximum_reduce_fusion
  261.6 0.7 broadcast_in_dim.96
  262.3 23.9 %all_to_all.22 = f32[64,1,1]{2,1,0:T(1,128)S(1)} all-to-all(f32[64,1,1]{2,1,0:T(1,128)S(1)} %broadcast_in_dim.96), channel_id=1, replica_groups=mesh['dp'=64,'mp'=8] {'dp'}, dimensions={0} | all-to-all | bytes 512 | tf_op jit(solution)/shard_map/all_to_all | solution.py:23
  286.2 0.7 reduce_sum.89
  (38 shorter events, 1.2 us)
Async XLA Ops:
  7.2 140.4 %all-gather.2.cloned.1.call-start = ((), (), s32[]{:S(2)}) async-start(), calls=%async_computation.4 | async-start | bytes 10649600 | tf_op jit(solution)/shard_map/all_gather | solution.py:17
  10.0 26.0 %collective-permute-start = (f32[1]{0:T(128)}, f32[1]{0:T(128)}, u32[]{:S(2)}, u32[]{:S(2)}) collective-permute-start(f32[1]{0:T(128)} %slice.142), channel_id=1, source_target_pairs={{8,0},{16,8},{24,16},{32,24},{40,32},{48,40},{56,48},{64,56},{72,6... | collective-permute-start | bytes 20 | tf_op jit(solution)/shard_map/ppermute | solution.py:44
  31.6 4.5 %copy-start.2 = (f32[512]{0:T(512)S(1)}, f32[512]{0:T(512)}, u32[]{:S(2)}) copy-start(f32[512]{0:T(512)} %param.17) | copy-start | bytes 6148
  31.6 4.5 %copy-start.3 = (f32[512]{0:T(512)S(1)}, f32[512]{0:T(512)}, u32[]{:S(2)}) copy-start(f32[512]{0:T(512)} %param.16) | copy-start | bytes 6148
  40.3 129.6 %all-to-all-start.2 = ((f32[64,2,1]{1,2,0:T(1,128)}), f32[64,2,1]{1,2,0:T(1,128)S(1)}, u32[]{:S(2)}, u32[]{:S(2)}) async-start(f32[64,2,1]{1,2,0:T(1,128)} %broadcast_in_dim.56), calls=%async_computation.2 | async-start | bytes 65536 | tf_op jit(solution)/shard_map/all_to_all | solution.py:23
  147.6 4.8 %copy-start = (bf16[512,4096]{0,1:T(8,128)(2,1)S(1)}, bf16[512,4096]{0,1:T(8,128)(2,1)}, u32[]{:S(2)}) copy-start(bf16[512,4096]{0,1:T(8,128)(2,1)} %copy.48) | copy-start | bytes 12582916
  160.2 2.1 copy-start.1
  172.4 57.3 %all-to-all-start = ((bf16[8,512,512]{1,2,0:T(8,128)(2,1)}), bf16[8,512,512]{1,2,0:T(8,128)(2,1)}, u32[]{:S(2)}, u32[]{:S(2)}) async-start(bf16[8,512,512]{1,2,0:T(8,128)(2,1)} %stack.3), calls=%async_computation | async-start | bytes 8388608 | tf_op jit(solution)/shard_map/all_to_all | solution.py:145
  178.5 51.2 %copy-start.4 = (f32[512]{0:T(512)S(1)}, f32[512]{0:T(512)}, u32[]{:S(2)}) copy-start(f32[512]{0:T(512)} %param.15) | copy-start | bytes 6148
  236.5 23.2 %all-to-all-start.1 = ((f32[8,1,1024]{2,1,0:T(1,128)}), f32[8,1,1024]{2,1,0:T(1,128)S(1)}, u32[]{:S(2)}, u32[]{:S(2)}) async-start(f32[8,1,1024]{2,1,0:T(1,128)} %broadcast_in_dim.51), calls=%async_computation.1 | async-start | bytes 65536 | tf_op jit(solution)/shard_map/all_to_all | solution.py:23
Sparse Core Ops, SparseCore 0:
  10.1 137.3 all-gather.1
